TPU v7x, 32 devices: a whole 2x2x4 slice. The times are simulated.
32 devices in a mesh: expert: 2 (over y), dp: 4 (over x, core), shard: 4 (over z).
Axes of the slice: x: 2, y: 2, z: 4, core: 2. Of those that a mesh axis runs over, the one named last changes fastest.
Arguments:
- grad_partials: bfloat16 [4, 2, 4096, 1536], P('dp', 'expert', 'shard'), may hold values from -120 to 120
- momentum: float32 [2, 4, 1024, 1536], P('expert', 'shard', 'dp'), may hold values from -3 to 3
- q_factor: float32 [1536, 2, 384], P(('dp', 'shard'), 'expert'), may hold values from -0.15625 to 0.15625
Outputs:
- next_momentum: float32 [2, 4, 1024, 1536], P('expert', 'shard', 'dp')
- next_factor: float32 [1536, 2, 384], P(('dp', 'shard'), 'expert')
- weight_update: bfloat16 [2, 4096, 1536], P('expert', 'shard')
All inputs are finite; a program needn't handle non-finite values.
Results may differ from a plain program's by a relative error of at most 0.015.
Values may be sent and summed in bfloat16 or wider, within the bound.
A program may use at most 64 MiB of HBM per device.

v0:
```python
import math
import jax
import jax.numpy as jnp
from jax import lax
from jax.sharding import PartitionSpec as P

clip_rms = 0.5
keep_share = 0.95
highest = lax.Precision.HIGHEST


def orthonormal(projected):
    gram_matrix = lax.psum(
        jnp.einsum("emr,ems->ers", projected, projected, precision=highest), ("dp", "shard")
    )
    triangles = jnp.linalg.cholesky(gram_matrix)

    def solve_one(triangle, columns):
        return jax.scipy.linalg.solve_triangular(triangle, columns.T, lower=True).T

    return jax.vmap(solve_one)(triangles, projected)


def shards(grad_partials, momentum, q_factor):
    partial_value = grad_partials[0]
    gradient = lax.psum_scatter(partial_value, "dp", scatter_dimension=1, tiled=True).astype(
        jnp.float32
    )
    momentum_rows = momentum[:, 0]
    experts, local_rows, hidden_width = gradient.shape
    factor_count, _, rank_width = q_factor.shape
    total_rows = local_rows * lax.axis_size("dp") * lax.axis_size("shard")
    entries = float(experts * lax.axis_size("expert") * total_rows * hidden_width)
    square_sum = lax.psum(jnp.sum(gradient * gradient), ("expert", "dp", "shard"))
    clip_scale = clip_rms / jnp.sqrt(square_sum / entries + 1e-06)
    buffer = momentum_rows + clip_scale * gradient
    zeros_init = jnp.zeros((experts, local_rows, rank_width), jnp.float32)
    projected = zeros_init + jnp.einsum(
        "emf,fer->emr",
        buffer,
        lax.all_gather(q_factor.astype(jnp.bfloat16), ("dp", "shard"), axis=0, tiled=True).astype(
            jnp.float32
        ),
        precision=highest,
    )
    ortho_basis = orthonormal(projected)
    right_term = jnp.einsum("emf,emr->fer", buffer, ortho_basis, precision=highest)
    right_factor = lax.psum(right_term, ("dp", "shard"))
    inverse = lax.rsqrt(jnp.sum(right_factor * right_factor, axis=0) + 1e-06)
    offset = (
        lax.axis_index("dp") * lax.axis_size("shard") + lax.axis_index("shard")
    ) * factor_count
    next_factor = lax.dynamic_slice_in_dim(right_factor, offset, factor_count, 0) * inverse[None]
    correction = jnp.einsum("emr,fer->emf", ortho_basis, right_factor, precision=highest)
    direction = jnp.einsum(
        "emr,fer->emf", ortho_basis * inverse[:, None, :], right_factor, precision=highest
    )
    next_momentum = (buffer - (1.0 - keep_share) * correction)[:, None]
    unit_scale = math.sqrt(total_rows * hidden_width / rank_width)
    local_update = (unit_scale * direction).astype(jnp.bfloat16)
    weight_update = lax.all_gather(local_update, "dp", axis=1, tiled=True)
    return (next_momentum, next_factor, weight_update)


def solution(mesh):
    placed = (
        P("dp", "expert", "shard", None),
        P("expert", "shard", "dp", None),
        P(("dp", "shard"), "expert", None),
    )
    return jax.shard_map(
        shards,
        mesh=mesh,
        in_specs=placed,
        out_specs=(
            P("expert", "shard", "dp", None),
            P(("dp", "shard"), "expert", None),
            P("expert", "shard", None),
        ),
        check_vma=False,
    )
```

profile of v0, /device:TPU:0, one launch (start us, length us, event | category | flops | bytes accessed | tf_op | source)
XLA Modules:
  0.0 446.0 jit_solution(1453472707407732005)
XLA Ops:
  8.1 0.7 reduce-scatter.2.cloned.1.call-update
  8.8 0.2 copy-done.5
  9.0 0.6 copy.21
  9.7 42.6 %reduce-scatter.2.cloned.1.call-done = bf16[1,256,1536]{2,1,0:T(8,128)(2,1)} async-done(((bf16[1,1024,1536]{2,1,0:T(8,128)(2,1)}), bf16[1,256,1536]{2,1,0:T(8,128)(2,1)}) %reduce-scatter.2.cloned.1.call-update) | async-done | bytes 786448 | tf_op jit(solution)/shard_map/reduce_scatter | solution.py:26
  52.3 2.1 fusion.6
  54.5 39.5 %psum.21 = f32[]{:T(128)} all-reduce(f32[]{:T(128)} %fusion.6), channel_id=1, replica_groups=mesh['expert'=2,'dp'=4,'shard'=4] {'expert','dp','shard'}, use_global_device_ids=true, to_apply=%region_2.0 | all-reduce | flops 1 | bytes 8 | tf_op jit(solution)/shard_map/psum | solution.py:34
  94.7 2.9 fusion.9
  97.6 1.6 convolution_bitcast_fusion.1
  99.3 0.2 all-reduce.6.cloned.1.call-start
  99.5 92.3 %all-reduce.4.cloned.1.call-done = f32[1,384,384]{1,2,0:T(8,128)} async-done(((f32[1,384,384]{1,2,0:T(8,128)}), f32[1,384,384]{1,2,0:T(8,128)}) %all-reduce.4.cloned.1.call-update) | async-done | bytes 589840 | tf_op jit(solution)/shard_map/psum | solution.py:13
  191.8 1.4 copy.13
  193.3 0.8 copy-done.4
  194.1 11.7 %custom-call.26 = f32[1,128,128]{2,1,0:T(8,128)S(1)} custom-call(f32[1,128,128]{2,1,0:T(8,128)S(1)} %cholesky.192), custom_call_target="Cholesky" | custom-call | tf_op jit(solution)/shard_map/jit(cholesky)/cholesky | solution.py:16
  205.9 9.8 %custom-call.27 = f32[1,1,128,128]{2,3,1,0:T(8,128)S(1)} custom-call(f32[1,1,128,128]{3,2,1,0:T(8,128)S(1)} %get-tuple-element.33), custom_call_target="InvertDiagBlocksLowerTriangular" | custom-call | tf_op jit(solution)/shard_map/jit(cholesky)/cholesky | solution.py:16
  215.7 1.2 constant_dynamic-update-slice_fusion.2
  216.9 1.2 fusion.12
  218.1 11.7 %custom-call.28 = f32[1,128,128]{2,1,0:T(8,128)S(1)} custom-call(f32[1,128,128]{2,1,0:T(8,128)S(1)} %cholesky.196), custom_call_target="Cholesky" | custom-call | tf_op jit(solution)/shard_map/jit(cholesky)/cholesky | solution.py:16
  229.9 10.0 %custom-call.29 = f32[1,1,128,128]{2,3,1,0:T(8,128)S(1)} custom-call(f32[1,1,128,128]{3,2,1,0:T(8,128)S(1)} %get-tuple-element.30), custom_call_target="InvertDiagBlocksLowerTriangular" | custom-call | tf_op jit(solution)/shard_map/jit(cholesky)/cholesky | solution.py:16
  239.9 0.2 fusion.17
  240.1 1.1 fusion.18
  241.2 11.7 %custom-call.30 = f32[1,128,128]{2,1,0:T(8,128)S(1)} custom-call(f32[1,128,128]{2,1,0:T(8,128)S(1)} %fusion.18), custom_call_target="Cholesky" | custom-call | tf_op jit(solution)/shard_map/jit(cholesky)/cholesky | solution.py:16
  252.9 0.7 compare_reduce_fusion
  253.7 0.6 compare_reduce_fusion.1
  256.3 0.9 select_select_fusion
  257.2 9.0 %while.1 = (s32[]{:T(128)}, f32[1,384,384]{2,1,0:T(8,128)}, s32[3,2]{0,1:T(2,128)S(1)}, f32[3,1,128,128]{3,2,1,0:T(8,128)S(1)}, s32[]{:T(128)}) while((s32[]{:T(128)}, f32[1,384,384]{2,1,0:T(8,128)}, s32[3,2]{0,1:T(2,128)S(1)}, f32[3,1,128,128]{3,2,1,0:T(8,128)S(1)}, s32[]{:T(128)}) %tuple.31), condition=%wide.while_cond, body=%wide.while_body.sunk | while | flops 2 | bytes 131189 | solution.py:19
  257.2 0.6 fusion.45
  257.8 2.3 bitcast_dynamic-update-slice_fusion.2
  260.3 0.6 fusion.45
  260.9 2.3 bitcast_dynamic-update-slice_fusion.2
  263.3 0.6 fusion.45
  263.9 2.3 bitcast_dynamic-update-slice_fusion.2
  266.2 29.5 %custom-call.31 = f32[1,3,128,128]{2,3,1,0:T(8,128)S(1)} custom-call(f32[1,3,128,128]{3,2,1,0:T(8,128)S(1)} %bitcast.165), custom_call_target="InvertDiagBlocksLowerTriangular" | custom-call | tf_op jit(solution)/shard_map/vmap(jit(_solve_triangular))/triangular_solve | solution.py:19
  295.7 0.3 fusion.29
  296.0 1.2 fusion.14
  297.2 0.3 convolution_bitcast_fusion.4
  297.5 1.5 fusion.16
  299.0 0.3 convolution_bitcast_fusion.3
  299.4 3.5 convolution_bitcast_fusion
  302.9 0.3 all-gather.6.cloned.1.call-start
  303.2 97.9 %all-reduce.6.cloned.1.call-done = f32[1536,1,384]{0,2,1:T(8,128)} async-done(((f32[1536,1,384]{0,2,1:T(8,128)}), f32[1536,1,384]{0,2,1:T(8,128)}) %all-reduce.6.cloned.1.call-update) | async-done | bytes 2359312 | tf_op jit(solution)/shard_map/psum | solution.py:48
  401.1 2.0 multiply_reduce_fusion
  403.2 0.3 copy-done
  403.5 3.7 fusion.3
  407.2 0.9 dynamic-slice_multiply_fusion
  408.1 1.7 copy.16
  409.8 5.3 %fusion.2 = f32[1,1,256,1536]{3,2,1,0:T(8,128)} fusion(f32[1536,1,384]{0,2,1:T(8,128)S(1)} %copy-done, bf16[1,256,1536]{2,1,0:T(8,128)(2,1)S(1)} %copy-done.2, f32[]{:T(128)S(6)} %div.15, f32[1,1,256,1536]{3,2,1,0:T(8,128)} %param.4, f32[1,128,256]{2,1,0:T(8,128)S(1)} %convolution_bitcast_fusion.3, f32[1,128,256]{2,1,0:T(8,128)S(1)} %convolution_bitcast_fusion.4, ...), kind=kOutput, calls=%fused_computation.7 | convolution fusion | flops 1814102016 | bytes 6684676 | tf_op jit(solution)/shard_map/emr,fer->emf/dot_general | solution.py:54
  415.1 19.6 %all-gather.6.cloned.1.call-done = bf16[1024,1536]{1,0:T(8,128)(2,1)} async-done(((bf16[256,1536]{1,0:T(8,128)(2,1)}), bf16[1024,1536]{1,0:T(8,128)(2,1)}) %all-gather.6.cloned.1.call-update) | async-done | bytes 3145744 | tf_op jit(solution)/shard_map/all_gather | solution.py:61
  434.7 3.8 copy.36
  (31 shorter events, 0.7 us)
Async XLA Ops:
  8.0 44.3 %reduce-scatter.2.cloned.1.call-start = ((), (), s32[]{:S(2)}) async-start(), calls=%async_computation.1 | async-start | bytes 3932160 | tf_op jit(solution)/shard_map/reduce_scatter | solution.py:26
  8.0 0.9 copy-start.5
  8.1 86.6 %copy-start.1 = (f32[1,1,256,1536]{3,2,1,0:T(8,128)S(1)}, f32[1,1,256,1536]{3,2,1,0:T(8,128)}, u32[]{:S(2)}) copy-start(f32[1,1,256,1536]{3,2,1,0:T(8,128)} %param.4) | copy-start | bytes 4718596
  8.7 85.9 %all-gather.4.cloned.1.call-start = ((), (), s32[]{:S(2)}) async-start(), calls=%async_computation.2 | async-start | bytes 1253376 | tf_op jit(solution)/shard_map/all_gather | solution.py:41
  9.6 182.2 %all-reduce.4.cloned.1.call-start = ((), (), s32[]{:S(2)}) async-start(), calls=%async_computation.3 | async-start | bytes 1179648 | tf_op jit(solution)/shard_map/psum | solution.py:13
  99.3 301.9 %all-reduce.6.cloned.1.call-start = ((), (), s32[]{:S(2)}) async-start(), calls=%async_computation.4 | async-start | bytes 4718592 | tf_op jit(solution)/shard_map/psum | solution.py:48
  191.8 1.4 copy-start.3
  193.3 0.8 copy-start.4
  257.1 42.2 %copy-start.2 = (bf16[1,256,1536]{2,1,0:T(8,128)(2,1)S(1)}, bf16[1,256,1536]{2,1,0:T(8,128)(2,1)}, u32[]{:S(2)}) copy-start(bf16[1,256,1536]{2,1,0:T(8,128)(2,1)} %reduce-scatter.2.cloned.1.call-done) | copy-start | bytes 2359300
  302.9 131.8 %all-gather.6.cloned.1.call-start = ((), (), s32[]{:S(2)}) async-start(), calls=%async_computation.5 | async-start | bytes 3932160 | tf_op jit(solution)/shard_map/all_gather | solution.py:61
  401.1 2.4 copy-start
Sparse Core Ops, SparseCore 0:
  11.3 40.9 reduce-scatter.1
  407.3 27.3 all-gather.5
Sparse Core Ops, SparseCore 1:
  12.1 50.7 all-gather.3
  99.3 92.4 all-reduce.3
  303.0 98.1 all-reduce.5
where the time goes:
time: 447 us; the launch traced here: 446 us
  waiting for transfers between devices  253 us (57%)
  other arithmetic  91.9 us (21%)
  blocking collectives  39.5 us (9%)
  matrix products  24.4 us (5%)
  between operations  18.6 us (4%)
  local copies, waits for them, and re-layouts  17.8 us (4%)
    psum x1, waiting for transfers between devices, shards(): right_factor = lax.psum(right_term, ('dp', 'shard'))  97.9 us
    psum x1, waiting for transfers between devices, orthonormal(): lax.psum(jnp.einsum('emr,ems->ers', projected, projected, precision=highe...  92.3 us
    another operation x10, other arithmetic, orthonormal(): triangles = jnp.linalg.cholesky(gram_matrix)  56.4 us
    reduce_scatter x1, waiting for transfers between devices, shards(): lax.psum_scatter(partial_value, 'dp', scatter_dimension=1, tiled=True)  42.6 us
    psum x1, blocking collectives, shards(): lax.psum(jnp.sum(gradient * gradient), ('expert', 'dp', 'shard'))  39.5 us
    another operation x3, other arithmetic, solve_one(): return jax.scipy.linalg.solve_triangular(triangle, columns.T, lower=True).T  30.4 us
    all_gather x1, waiting for transfers between devices, shards(): weight_update = lax.all_gather(local_update, 'dp', axis=1, tiled=True)  19.6 us
    another operation x9, local copies, waits for them, and re-layouts  8.96 us
  transfers between devices with their start and end apart: 5, of which 4 were waited for; matrix products, arithmetic and copies ran while one was open for 2% of the time, Pallas kernels for 0%

commit v1 on v0

--- a/solution.py
+++ b/solution.py
@@ -45,7 +45,7 @@
     )
     ortho_basis = orthonormal(projected)
     right_term = jnp.einsum("emf,emr->fer", buffer, ortho_basis, precision=highest)
-    right_factor = lax.psum(right_term, ("dp", "shard"))
+    right_factor = lax.psum(lax.psum(right_term, "shard"), "dp")
     inverse = lax.rsqrt(jnp.sum(right_factor * right_factor, axis=0) + 1e-06)
     offset = (
         lax.axis_index("dp") * lax.axis_size("shard") + lax.axis_index("shard")

time: 447 us -> 498 us (1.11)
  waiting for transfers between devices: 253 us -> 305 us
    psum x1 -> x2, waiting for transfers between devices: 97.9 us -> 148 us  [shards(): right_factor = lax.psum(lax.psum(right_term, 'shard'), 'dp')]
  transfers between devices with their start and end apart: 5 -> 6, of which waited for: 4 -> 5; matrix products, arithmetic and copies ran while one was open for 2% -> 2% of each run, Pallas kernels for 0% -> 0%
where the time goes in v1:
time: 498 us; the launch traced here: 497 us
  waiting for transfers between devices  305 us (61%)
  other arithmetic  91.9 us (18%)
  blocking collectives  39.5 us (8%)
  matrix products  24.4 us (5%)
  between operations  18.3 us (4%)
  local copies, waits for them, and re-layouts  17.8 us (4%)
    psum x2, waiting for transfers between devices, shards(): right_factor = lax.psum(lax.psum(right_term, 'shard'), 'dp')  148 us
    psum x1, waiting for transfers between devices, orthonormal(): lax.psum(jnp.einsum('emr,ems->ers', projected, projected, precision=highe...  92.3 us
    another operation x10, other arithmetic, orthonormal(): triangles = jnp.linalg.cholesky(gram_matrix)  56.4 us
    reduce_scatter x1, waiting for transfers between devices, shards(): lax.psum_scatter(partial_value, 'dp', scatter_dimension=1, tiled=True)  42.6 us
    psum x1, blocking collectives, shards(): lax.psum(jnp.sum(gradient * gradient), ('expert', 'dp', 'shard'))  39.5 us
    another operation x3, other arithmetic, solve_one(): return jax.scipy.linalg.solve_triangular(triangle, columns.T, lower=True).T  30.4 us
    all_gather x1, waiting for transfers between devices, shards(): weight_update = lax.all_gather(local_update, 'dp', axis=1, tiled=True)  20.9 us
  transfers between devices with their start and end apart: 6, of which 5 were waited for; matrix products, arithmetic and copies ran while one was open for 2% of the time, Pallas kernels for 0%

profile of v1, /device:TPU:0, one launch (start us, length us, event | category | flops | bytes accessed | tf_op | source)
XLA Modules:
  0.0 497.3 jit_solution(8432761840672657679)
XLA Ops:
  8.1 0.7 reduce-scatter.2.cloned.1.call-update
  9.0 0.6 copy.21
  9.7 42.6 %reduce-scatter.2.cloned.1.call-done = bf16[1,256,1536]{2,1,0:T(8,128)(2,1)} async-done(((bf16[1,1024,1536]{2,1,0:T(8,128)(2,1)}), bf16[1,256,1536]{2,1,0:T(8,128)(2,1)}) %reduce-scatter.2.cloned.1.call-update) | async-done | bytes 786448 | tf_op jit(solution)/shard_map/reduce_scatter | solution.py:26
  52.3 2.1 fusion.6
  54.5 39.5 %psum.28 = f32[]{:T(128)} all-reduce(f32[]{:T(128)} %fusion.6), channel_id=1, replica_groups=mesh['expert'=2,'dp'=4,'shard'=4] {'expert','dp','shard'}, use_global_device_ids=true, to_apply=%region_2.0 | all-reduce | flops 1 | bytes 8 | tf_op jit(solution)/shard_map/psum | solution.py:34
  94.7 2.9 fusion.9
  97.6 1.6 convolution_bitcast_fusion.1
  99.3 0.2 all-reduce.7.cloned.1.call-start
  99.5 92.3 %all-reduce.5.cloned.1.call-done = f32[1,384,384]{1,2,0:T(8,128)} async-done(((f32[1,384,384]{1,2,0:T(8,128)}), f32[1,384,384]{1,2,0:T(8,128)}) %all-reduce.5.cloned.1.call-update) | async-done | bytes 589840 | tf_op jit(solution)/shard_map/psum | solution.py:13
  191.9 1.4 copy.13
  193.3 0.8 copy-done.4
  194.1 11.7 %custom-call.26 = f32[1,128,128]{2,1,0:T(8,128)S(1)} custom-call(f32[1,128,128]{2,1,0:T(8,128)S(1)} %cholesky.192), custom_call_target="Cholesky" | custom-call | tf_op jit(solution)/shard_map/jit(cholesky)/cholesky | solution.py:16
  205.9 9.8 %custom-call.27 = f32[1,1,128,128]{2,3,1,0:T(8,128)S(1)} custom-call(f32[1,1,128,128]{3,2,1,0:T(8,128)S(1)} %get-tuple-element.33), custom_call_target="InvertDiagBlocksLowerTriangular" | custom-call | tf_op jit(solution)/shard_map/jit(cholesky)/cholesky | solution.py:16
  215.7 1.2 constant_dynamic-update-slice_fusion.2
  216.9 1.2 fusion.12
  218.1 11.7 %custom-call.28 = f32[1,128,128]{2,1,0:T(8,128)S(1)} custom-call(f32[1,128,128]{2,1,0:T(8,128)S(1)} %cholesky.196), custom_call_target="Cholesky" | custom-call | tf_op jit(solution)/shard_map/jit(cholesky)/cholesky | solution.py:16
  229.9 10.0 %custom-call.29 = f32[1,1,128,128]{2,3,1,0:T(8,128)S(1)} custom-call(f32[1,1,128,128]{3,2,1,0:T(8,128)S(1)} %get-tuple-element.30), custom_call_target="InvertDiagBlocksLowerTriangular" | custom-call | tf_op jit(solution)/shard_map/jit(cholesky)/cholesky | solution.py:16
  239.9 0.2 fusion.17
  240.1 1.1 fusion.18
  241.2 11.7 %custom-call.30 = f32[1,128,128]{2,1,0:T(8,128)S(1)} custom-call(f32[1,128,128]{2,1,0:T(8,128)S(1)} %fusion.18), custom_call_target="Cholesky" | custom-call | tf_op jit(solution)/shard_map/jit(cholesky)/cholesky | solution.py:16
  252.9 0.7 compare_reduce_fusion
  253.7 0.6 compare_reduce_fusion.1
  256.3 0.9 select_select_fusion
  257.2 9.0 %while.1 = (s32[]{:T(128)}, f32[1,384,384]{2,1,0:T(8,128)}, s32[3,2]{0,1:T(2,128)S(1)}, f32[3,1,128,128]{3,2,1,0:T(8,128)S(1)}, s32[]{:T(128)}) while((s32[]{:T(128)}, f32[1,384,384]{2,1,0:T(8,128)}, s32[3,2]{0,1:T(2,128)S(1)}, f32[3,1,128,128]{3,2,1,0:T(8,128)S(1)}, s32[]{:T(128)}) %tuple.31), condition=%wide.while_cond, body=%wide.while_body.sunk | while | flops 2 | bytes 131189 | solution.py:19
  257.2 0.6 fusion.45
  257.8 2.3 bitcast_dynamic-update-slice_fusion.2
  260.3 0.6 fusion.45
  260.9 2.3 bitcast_dynamic-update-slice_fusion.2
  263.3 0.6 fusion.45
  263.9 2.3 bitcast_dynamic-update-slice_fusion.2
  266.2 29.5 %custom-call.31 = f32[1,3,128,128]{2,3,1,0:T(8,128)S(1)} custom-call(f32[1,3,128,128]{3,2,1,0:T(8,128)S(1)} %bitcast.165), custom_call_target="InvertDiagBlocksLowerTriangular" | custom-call | tf_op jit(solution)/shard_map/vmap(jit(_solve_triangular))/triangular_solve | solution.py:19
  295.7 0.3 fusion.29
  296.0 1.2 fusion.14
  297.2 0.3 convolution_bitcast_fusion.4
  297.5 1.5 fusion.16
  299.1 0.3 convolution_bitcast_fusion.3
  299.4 3.5 convolution_bitcast_fusion
  303.0 93.6 %all-reduce.7.cloned.1.call-done = f32[1536,1,384]{0,2,1:T(8,128)} async-done(((f32[1536,1,384]{0,2,1:T(8,128)}), f32[1536,1,384]{0,2,1:T(8,128)}) %all-reduce.7.cloned.1.call-update) | async-done | bytes 2359312 | tf_op jit(solution)/shard_map/psum | solution.py:48
  396.6 0.3 all-gather.6.cloned.1.call-start
  396.9 54.5 %all-reduce.9.cloned.1.call-done = f32[1536,1,384]{0,2,1:T(8,128)} async-done(((f32[1536,1,384]{0,2,1:T(8,128)}), f32[1536,1,384]{0,2,1:T(8,128)}) %all-reduce.9.cloned.1.call-update) | async-done | bytes 2359312 | tf_op jit(solution)/shard_map/psum | solution.py:48
  451.4 2.0 multiply_reduce_fusion
  453.5 0.3 copy-done
  453.8 3.7 fusion.3
  457.5 0.9 dynamic-slice_multiply_fusion
  458.3 1.7 copy.16
  460.1 5.3 %fusion.2 = f32[1,1,256,1536]{3,2,1,0:T(8,128)} fusion(f32[1536,1,384]{0,2,1:T(8,128)S(1)} %copy-done, bf16[1,256,1536]{2,1,0:T(8,128)(2,1)S(1)} %copy-done.2, f32[]{:T(128)S(6)} %div.15, f32[1,1,256,1536]{3,2,1,0:T(8,128)} %param.4, f32[1,128,256]{2,1,0:T(8,128)S(1)} %convolution_bitcast_fusion.3, f32[1,128,256]{2,1,0:T(8,128)S(1)} %convolution_bitcast_fusion.4, ...), kind=kOutput, calls=%fused_computation.7 | convolution fusion | flops 1814102016 | bytes 6684676 | tf_op jit(solution)/shard_map/emr,fer->emf/dot_general | solution.py:54
  465.4 20.9 %all-gather.6.cloned.1.call-done = bf16[1024,1536]{1,0:T(8,128)(2,1)} async-done(((bf16[256,1536]{1,0:T(8,128)(2,1)}), bf16[1024,1536]{1,0:T(8,128)(2,1)}) %all-gather.6.cloned.1.call-update) | async-done | bytes 3145744 | tf_op jit(solution)/shard_map/all_gather | solution.py:61
  486.2 3.8 copy.37
  (34 shorter events, 0.9 us)
Async XLA Ops:
  8.0 44.3 %reduce-scatter.2.cloned.1.call-start = ((), (), s32[]{:S(2)}) async-start(), calls=%async_computation.1 | async-start | bytes 3932160 | tf_op jit(solution)/shard_map/reduce_scatter | solution.py:26
  8.0 0.9 copy-start.5
  8.1 86.6 %copy-start.1 = (f32[1,1,256,1536]{3,2,1,0:T(8,128)S(1)}, f32[1,1,256,1536]{3,2,1,0:T(8,128)}, u32[]{:S(2)}) copy-start(f32[1,1,256,1536]{3,2,1,0:T(8,128)} %param.4) | copy-start | bytes 4718596
  8.7 85.9 %all-gather.4.cloned.1.call-start = ((), (), s32[]{:S(2)}) async-start(), calls=%async_computation.2 | async-start | bytes 1253376 | tf_op jit(solution)/shard_map/all_gather | solution.py:41
  9.6 182.2 %all-reduce.5.cloned.1.call-start = ((), (), s32[]{:S(2)}) async-start(), calls=%async_computation.3 | async-start | bytes 1179648 | tf_op jit(solution)/shard_map/psum | solution.py:13
  99.3 297.3 %all-reduce.7.cloned.1.call-start = ((), (), s32[]{:S(2)}) async-start(), calls=%async_computation.4 | async-start | bytes 4718592 | tf_op jit(solution)/shard_map/psum | solution.py:48
  191.9 1.4 copy-start.3
  193.3 0.8 copy-start.4
  257.2 42.2 %copy-start.2 = (bf16[1,256,1536]{2,1,0:T(8,128)(2,1)S(1)}, bf16[1,256,1536]{2,1,0:T(8,128)(2,1)}, u32[]{:S(2)}) copy-start(bf16[1,256,1536]{2,1,0:T(8,128)(2,1)} %reduce-scatter.2.cloned.1.call-done) | copy-start | bytes 2359300
  302.9 148.5 %all-reduce.9.cloned.1.call-start = ((), (), s32[]{:S(2)}) async-start(), calls=%async_computation.5 | async-start | bytes 4718592 | tf_op jit(solution)/shard_map/psum | solution.py:48
  396.6 89.7 %all-gather.6.cloned.1.call-start = ((), (), s32[]{:S(2)}) async-start(), calls=%async_computation.6 | async-start | bytes 3932160 | tf_op jit(solution)/shard_map/all_gather | solution.py:61
  451.4 2.4 copy-start
Sparse Core Ops, SparseCore 0:
  11.3 40.9 reduce-scatter.1
  396.7 54.6 all-reduce.8
  457.6 28.5 all-gather.5
Sparse Core Ops, SparseCore 1:
  12.1 50.7 all-gather.3
  99.3 92.4 all-reduce.4
  303.0 93.5 all-reduce.6
